TPU v7x, 128 devices: a whole 4x4x4 slice. The times are simulated.
128 devices in a mesh: light: 8 (over x, z_hi), screen: 16 (over y, z_lo, core).
Axes of the slice: x: 4, y: 4, z: 4 (z_hi: 2, z_lo: 2; z = z_hi * 2 + z_lo), core: 2. Of those that a mesh axis runs over, the one named last changes fastest.
Arguments:
- density: float32 [256, 512, 1024], P('screen', None, 'light'), may hold values from 0 to 1.046875, as said below
- albedo: float32 [256, 512, 1024], P('screen', None, 'light'), may hold values from 0.2 to 1
- light_in: float32 [256, 512], replicated, may hold values from 0.5 to 1.5
- occupancy: int32 [16, 32, 64], P('screen', None, 'light'), may hold values 0 or 1
- phase: int32 [512, 1024], replicated, may hold values from 0 to 15
- fractions: float32 [3, 16], replicated, may hold values from 0 to 1
Outputs:
- image: float32 [512, 1024], P('screen', 'light')
- transmittance: float32 [512, 1024], P('screen', 'light')
- lit_bricks: float32 [256, 512, 1024], P('light', 'screen')
Inputs may be any that keep to these rules, and one draw needn't show every extreme that they name: `density`: nonnegative extinction of each cell. `occupancy`: 1 where the brick of 16 cells on a side is occupied.
All inputs are finite; a program needn't handle non-finite values. No bound on the sum of `occupancy` on one device may be relied on, other than what follows from the above.
Results may differ from a plain program's by a relative error of at most 0.0003.
Values sent between devices are 32-bit elements; how exact they have to be, the bound alone decides.
A program may use at most 192 MiB of HBM per device.

v0:
```python
import jax
import jax.numpy as jnp
from jax import lax
from jax.sharding import PartitionSpec as P

BRICK = 16


def passed_along(value, axis, by):
    peers = lax.axis_size(axis)
    pairs = [(i, i + by) for i in range(peers) if 0 <= i + by < peers]
    return lax.ppermute(value, axis, pairs)


def from_everyone(value, axis):
    copies = jnp.broadcast_to(value, (lax.axis_size(axis), *value.shape))
    return lax.all_to_all(copies, axis, split_axis=0, concat_axis=0, tiled=True)


def combined_pairwise(pieces, combine):
    while len(jax.tree.leaves(pieces)[0]) > 1:
        pieces = jax.vmap(combine)(*(pieces[side::2] for side in (0, 1)))
    return pieces[0]


def prefix(value, axis, combine, identity):
    peers, index = (lax.axis_size(axis), lax.axis_index(axis))
    passed = jnp.arange(peers) < index

    def kept(part, zero, own):
        part = jnp.where(
            passed.reshape(-1, *(1 for _ in own.shape)), part, jnp.asarray(zero, own.dtype)
        )
        return part

    pieces = from_everyone(value, axis)
    return combined_pairwise(kept(pieces, identity, value), combine)


def in_blocks(value, dim, peers):
    dims = value.shape
    parts = value.reshape(*dims[:dim], peers, dims[dim] // peers, *dims[dim + 1 :])
    return jnp.moveaxis(parts, dim, 0)


def piece_ends(length, count):
    unit = 8 if length >= 8 * count else 1
    return [length // unit * k // count * unit for k in range(1, count)]


def in_order(parts, dim):
    parts = jnp.moveaxis(parts, 0, dim)
    dims = parts.shape
    return parts.reshape(*dims[:dim], dims[dim] * dims[dim + 1], *dims[dim + 2 :])


def several_exchanges(value, axis, pieces, split_dim, concat_dim):
    parts = in_blocks(value, split_dim, lax.axis_size(axis))
    widest = max(range(1, max(2, parts.ndim - 1)), key=lambda d: parts.shape[d])
    finished = []
    for piece in jnp.split(parts, piece_ends(parts.shape[widest], pieces), axis=widest):
        if piece.size:
            finished.append(lax.all_to_all(piece, axis, split_axis=0, concat_axis=0, tiled=True))
    return in_order(jnp.concatenate(finished, axis=widest), concat_dim)


def prefix_last(values):
    length = values.shape[-1]
    block = 128
    count = length // block
    shaped = values.reshape(values.shape[:-1] + (count, block))
    rowsidx = lax.broadcasted_iota(jnp.int32, (block, block), 0)
    colsidx = lax.broadcasted_iota(jnp.int32, (block, block), 1)
    upper = (rowsidx < colsidx).astype(jnp.float32)
    within = jnp.matmul(shaped, upper, precision=lax.Precision.HIGHEST)
    totals = jnp.sum(shaped, axis=-1)
    carried = jnp.cumsum(totals, axis=-1) - totals
    return (within + carried[..., None]).reshape(values.shape)


def prefix_first(values):
    length = values.shape[0]
    count = length // length
    shaped = values.reshape(count, length, -1)
    rowsidx = lax.broadcasted_iota(jnp.int32, (length, length), 0)
    colsidx = lax.broadcasted_iota(jnp.int32, (length, length), 1)
    lower = (colsidx < rowsidx).astype(jnp.float32)
    within = jnp.einsum("ij,bjr->bir", lower, shaped, precision=lax.Precision.HIGHEST)
    totals = jnp.sum(shaped, axis=1)
    carried = jnp.cumsum(totals, axis=0) - totals
    return (within + carried[:, None]).reshape(values.shape)


def corner_fractions(rays, fractions):
    levels = lax.broadcasted_iota(jnp.int32, (fractions.shape[1], 1, 1), 0)
    onehot = (rays[None] == levels).astype(jnp.float32)
    return jnp.einsum("kp,prc->krc", fractions, onehot, precision=lax.Precision.HIGHEST)


def resample(field, tail, weights, deep, cols):
    first = field[:, 0:cols]
    second = field[:, 1 : cols + 1]
    edge_first = tail[:, 0:cols]
    edge_second = tail[:, 1 : cols + 1]
    first_next = jnp.concatenate([first[:, :, 1:], edge_first], axis=2)
    second_next = jnp.concatenate([second[:, :, 1:], edge_second], axis=2)
    depth_w = weights[0]
    column_w = weights[1]
    light_w = weights[2]
    near = first + column_w * (second - first)
    further = first_next + column_w * (second_next - first_next)
    mixed = near + light_w * (further - near)
    lower = mixed[0:deep]
    higher = mixed[1 : deep + 1]
    return lower + depth_w * (higher - lower)


def composite(extinct, shaded):
    screened = prefix_first(extinct)
    part = jnp.sum(jnp.exp(-screened) * (1.0 - jnp.exp(-extinct)) * shaded, axis=0)
    return (part, jnp.sum(extinct, axis=0))


def finish(parts, totals):
    before = jnp.cumsum(totals, axis=0) - totals
    picture = jnp.sum(jnp.exp(-before) * parts, axis=0)
    return (picture, jnp.exp(-jnp.sum(totals, axis=0)))


def march_slabs(masked, lit, phase, fractions):
    slab_b, width_a, slab_l = masked.shape
    light_idx = lax.axis_index("light")
    rims = passed_along((masked[:2], lit[:2]), "screen", -1)
    dens_ext = jnp.pad(jnp.concatenate([masked, rims[0]], axis=0), ((0, 0), (0, 2), (0, 0)))
    lit_ext = jnp.pad(jnp.concatenate([lit, rims[1]], axis=0), ((0, 0), (0, 2), (0, 0)))
    tails = passed_along((dens_ext[:, :, :1], lit_ext[:, :, :1]), "light", -1)
    rays = lax.dynamic_slice_in_dim(phase, light_idx * slab_l, slab_l, 1)
    weights = corner_fractions(rays, fractions)
    extinct = resample(dens_ext, tails[0], weights, slab_b, width_a)
    shaded = resample(lit_ext, tails[1], weights, slab_b, width_a)
    part, total = composite(extinct, shaded)
    parts, totals = (
        lax.all_to_all(part[None], "screen", split_axis=1, concat_axis=0, tiled=True),
        lax.all_to_all(total[None], "screen", split_axis=1, concat_axis=0, tiled=True),
    )
    return finish(parts, totals)


def local(density, albedo, light_in, occupancy, phase, fractions):
    slab_b, width_a, slab_l = density.shape
    bricks_b, bricks_a, bricks_l = occupancy.shape
    masked = (
        density.reshape(bricks_b, BRICK, bricks_a, BRICK, bricks_l, BRICK)
        * occupancy.astype(jnp.float32)[:, None, :, None, :, None]
    ).reshape(density.shape)
    screen_idx = lax.axis_index("screen")
    local_depth = prefix_last(masked)
    totals = jnp.sum(masked, axis=2)
    before = prefix(totals, "light", jnp.add, jnp.zeros_like(totals))
    incoming = lax.dynamic_slice_in_dim(light_in, screen_idx * slab_b, slab_b, 0)
    lit = albedo * incoming[:, :, None] * jnp.exp(-(local_depth + before[:, :, None]))
    lit_cam = lax.all_to_all(lit, "screen", split_axis=1, concat_axis=0, tiled=True)
    lit_cam = several_exchanges(lit_cam, "light", 2, 0, 2)
    picture, passing = march_slabs(masked, lit, phase, fractions)
    return (picture, passing, lit_cam)


def solution(mesh):
    return jax.shard_map(
        local,
        mesh=mesh,
        in_specs=(
            P("screen", None, "light"),
            P("screen", None, "light"),
            P(),
            P("screen", None, "light"),
            P(),
            P(),
        ),
        out_specs=(P("screen", "light"), P("screen", "light"), P("light", "screen", None)),
        check_vma=False,
    )
```

profile of v0, /device:TPU:8, one launch (start us, length us, event | category | flops | bytes accessed | tf_op | source)
XLA Modules:
  0.0 294.9 jit_solution(8581806873530012763)
XLA Ops:
  0.6 0.8 convert_bitcast_fusion
  1.6 1.5 mul.120
  3.1 2.2 mul.121
  5.3 5.2 %fusion.36 = (f32[16,512]{1,0:T(8,128)S(1)}, f32[16,512,128]{2,1,0:T(8,128)}) fusion(f32[16,512,128]{2,1,0:T(8,128)} %param.6, f32[512,128]{1,0:T(8,128)S(1)} %mul.121), kind=kLoop, calls=%fused_computation.68 | loop fusion | flops 2088960 | bytes 8683520 | tf_op jit(solution)/shard_map/reduce_sum | solution.py:76
  11.2 7.6 %all-to-all-start.1 = ((f32[8,16,512]{2,1,0:T(8,128)}), f32[8,16,512]{2,1,0:T(8,128)S(1)}, u32[]{:S(2)}, u32[]{:S(2)}) async-start(f32[8,16,512]{2,1,0:T(8,128)} %broadcast_in_dim.29), calls=%async_computation.1 | async-start | bytes 524288 | tf_op jit(solution)/shard_map/all_to_all | solution.py:17
  18.9 19.6 %reshape.94 = f32[1,16,32,16,8,16]{5,4,3,2,1,0:T(8,128)} reshape(f32[16,512,128]{2,1,0:T(8,128)} %param.6) | data formatting | bytes 8388608 | tf_op jit(solution)/shard_map/reshape | solution.py:153
  38.4 4.8 %slice_multiply_fusion = f32[1,2,32,16,8,16]{5,4,3,2,1,0:T(8,128)} fusion(f32[1,16,32,16,8,16]{5,4,3,2,1,0:T(8,128)} %reshape.94, f32[32,8]{1,0:T(8,128)S(1)} %copy.28), kind=kLoop, calls=%fused_computation.40 | loop fusion | flops 131072 | bytes 1049600 | tf_op jit(solution)/shard_map/mul | solution.py:153
  43.3 3.9 %slice.94 = f32[2,512,128]{2,1,0:T(8,128)} reshape(f32[1,2,32,16,8,16]{5,4,3,2,1,0:T(8,128)} %slice_multiply_fusion) | data formatting | bytes 1048576 | tf_op jit(solution)/shard_map/slice | solution.py:133
  47.2 2.0 collective-permute-start
  50.0 1.3 fusion.28
  52.0 6.2 %exponential_multiply_fusion = f32[16,512,128]{2,1,0:T(8,128)S(1)} fusion(f32[16,512,128]{2,1,0:T(8,128)} %param.7, f32[16,512,128]{2,1,0:T(8,128)} %get-tuple-element.4, f32[16,512]{1,0:T(8,128)S(1)} %fusion.34, f32[16,512]{1,0:T(8,128)S(1)} %sub.66, f32[16,512]{1,0:T(8,128)S(1)} %constant_dynamic-slice_fusion), kind=kOutput, calls=%fused_computation.42 | convolution fusion | flops 1615872000 | bytes 12681216 | tf_op jit(solution)/shard_map/dot_general | solution.py:75
  58.3 4.4 %copy.36 = f32[16,512,128]{2,0,1:T(8,128)} copy(f32[16,512,128]{2,1,0:T(8,128)S(1)} %exponential_multiply_fusion) | data formatting | bytes 8388608 | tf_op jit(solution)/shard_map/mul | solution.py:161
  62.7 2.9 collective-permute-start.2
  65.6 5.5 %all-to-all-start.3 = ((f32[16,512,128]{2,0,1:T(8,128)}), f32[16,512,128]{2,0,1:T(8,128)}, u32[]{:S(2)}, u32[]{:S(2)}) async-start(f32[16,512,128]{2,0,1:T(8,128)} %copy.36), calls=%async_computation.3 | async-start | bytes 8388608 | tf_op jit(solution)/shard_map/all_to_all | solution.py:162
  71.1 2.5 pad_maximum_fusion
  73.6 2.7 pad_slice_fusion.5
  76.3 1.0 copy-done.2
  77.2 3.5 %pad_slice_fusion.4 = f32[18,512,127]{2,1,0:T(8,128)} fusion(f32[18,512,128]{2,1,0:T(8,128)S(1)} %pad_maximum_fusion), kind=kLoop, calls=%fused_computation.26 | loop fusion | bytes 9400320 | tf_op jit(solution)/shard_map/slice | solution.py:106
  80.8 3.4 %copy.30 = f32[18,514,1]{1,2,0:T(1,128)S(1)} copy(f32[18,514,1]{2,1,0:T(8,128)} %pad_slice_fusion.5) | data formatting | bytes 74016 | tf_op jit(solution)/shard_map/slice | solution.py:136
  84.2 1.3 collective-permute-start.1
  85.5 5.7 %fusion.4 = f32[18,512,127]{2,1,0:T(8,128)} fusion(f32[2,512,128]{2,1,0:T(8,128)S(1)} %collective-permute-done, f32[16,512,128]{2,1,0:T(8,128)} %get-tuple-element.4), kind=kLoop, calls=%fused_computation.9 | loop fusion | flops 1170432 | bytes 9400320 | tf_op jit(solution)/shard_map/concatenate | solution.py:134
  91.2 16.4 %collective-permute-done.1 = f32[18,514,1]{1,2,0:T(1,128)S(1)} collective-permute-done((f32[18,514,1]{1,2,0:T(1,128)S(1)}, f32[18,514,1]{1,2,0:T(1,128)S(1)}, u32[]{:S(2)}, u32[]{:S(2)}) %collective-permute-start.1) | collective-permute-done | bytes 37040 | tf_op jit(solution)/shard_map/ppermute | solution.py:12
  107.7 3.0 %copy.32 = f32[18,512,1]{2,1,0:T(8,128)} copy(f32[18,512,1]{1,2,0:T(1,128)S(1)} %get-tuple-element.16) | data formatting | bytes 73728 | tf_op jit(solution)/shard_map/slice | solution.py:104
  110.6 2.8 copy.31
  113.5 2.5 pad_maximum_fusion.1
  116.0 3.5 %pad_slice_fusion.2 = f32[18,512,127]{2,1,0:T(8,128)} fusion(f32[18,512,128]{2,1,0:T(8,128)S(1)} %pad_maximum_fusion.1), kind=kLoop, calls=%fused_computation.24 | loop fusion | bytes 9400320 | tf_op jit(solution)/shard_map/slice | solution.py:106
  119.5 2.5 pad_slice_fusion.3
  122.0 3.4 %copy.33 = f32[18,514,1]{1,2,0:T(1,128)S(1)} copy(f32[18,514,1]{2,1,0:T(8,128)} %pad_slice_fusion.3) | data formatting | bytes 74016 | tf_op jit(solution)/shard_map/slice | solution.py:136
  125.4 1.5 collective-permute-start.3
  126.9 5.6 %fusion.3 = f32[18,512,127]{2,1,0:T(8,128)} fusion(f32[2,512,128]{2,1,0:T(8,128)S(1)} %collective-permute-done.2, f32[16,512,128]{2,1,0:T(8,128)} %copy-done.4), kind=kLoop, calls=%fused_computation.8 | loop fusion | flops 1170432 | bytes 9400320 | tf_op jit(solution)/shard_map/concatenate | solution.py:135
  133.0 2.8 copy.35
  135.8 2.9 copy.34
  138.8 24.6 %fusion.14 = (f32[18,512,128]{2,1,0:T(8,128)}, f32[18,512,128]{2,1,0:T(8,128)S(1)}) fusion(f32[18,512,1]{2,1,0:T(8,128)} %copy.34, f32[18,512,127]{2,1,0:T(8,128)} %fusion.3, f32[18,512,1]{2,1,0:T(8,128)} %copy.35, f32[18,512,127]{2,1,0:T(8,128)} %pad_slice_fusion.2, f32[18,512,128]{2,1,0:T(8,128)} %copy-done.3, f32[512,128]{1,0:T(8,128)S(1)} %bitcast.69, ...), kind=kLoop, calls=%fused_computation.23 | loop fusion | flops 25952256 | bytes 38273024 | tf_op jit(solution)/shard_map/add | solution.py:112
  163.4 1.4 fusion.37
  164.8 1.1 subtract_bitcast_fusion
  165.9 0.9 copy-done.5
  166.8 4.8 %fusion.24 = f32[2,8,512,128]{3,1,2,0:T(8,128)S(1)} fusion(f32[2,8,512,128]{3,2,1,0:T(8,128)S(1)} %bitcast.63, f32[65536]{0:T(1024)S(1)} %subtract_bitcast_fusion), kind=kOutput, calls=%fused_computation.45 | convolution fusion | flops 203424000 | bytes 8650752 | tf_op jit(solution)/shard_map/ij,bjr->bir/dot_general | solution.py:88
  171.6 2.8 copy.43
  174.5 19.5 %all-to-all-start = ((f32[1,512,128]{2,0,1:T(1,128)}), f32[1,512,128]{2,0,1:T(1,128)S(1)}, u32[]{:S(2)}, u32[]{:S(2)}) async-start(f32[1,512,128]{2,0,1:T(1,128)} %bitcast.6), calls=%async_computation | async-start | bytes 524288 | tf_op jit(solution)/shard_map/all_to_all | solution.py:144
  194.0 7.4 %fusion.16 = f32[512,128]{1,0:T(8,128)} fusion(f32[2,8,512,128]{3,2,1,0:T(8,128)} %copy.43, f32[18,512,128]{2,1,0:T(8,128)} %get-tuple-element.12, f32[16,512,128]{2,1,0:T(8,128)} %copy-done.5, f32[512,128]{1,0:T(8,128)S(1)} %bitcast.68), kind=kLoop, calls=%fused_computation.30 | loop fusion | flops 8323072 | bytes 17301504 | tf_op jit(solution)/shard_map/reduce_sum | solution.py:120
  201.4 5.5 %copy.38 = f32[16,16,32,128]{3,2,1,0:T(8,128)} copy(f32[16,16,32,128]{3,1,2,0:T(8,128)} %bitcast.17) | data formatting | bytes 8388608 | tf_op jit(solution)/shard_map/all_to_all | solution.py:162
  206.9 5.7 %all-to-all-start.2 = ((f32[1,512,128]{2,0,1:T(1,128)}), f32[1,512,128]{2,0,1:T(1,128)S(1)}, u32[]{:S(2)}, u32[]{:S(2)}) async-start(f32[1,512,128]{2,0,1:T(1,128)} %bitcast.13), calls=%async_computation.2 | async-start | bytes 524288 | tf_op jit(solution)/shard_map/all_to_all | solution.py:143
  212.6 4.2 %fusion.39 = (f32[8,16,32,128]{3,2,1,0:T(8,128)S(1)}, f32[8,16,32,128]{3,2,1,0:T(8,128)}) fusion(f32[8,32,32,128]{3,2,1,0:T(8,128)} %bitcast.64), kind=kLoop, calls=%fused_computation.70 | loop fusion | bytes 8388608 | tf_op jit(solution)/shard_map/split | solution.py:61
  216.8 1.3 all-to-all-done.2
  218.1 36.9 %all_to_all.54 = f32[8,16,32,128]{3,2,1,0:T(8,128)} all-to-all(f32[8,16,32,128]{3,2,1,0:T(8,128)S(1)} %get-tuple-element.7), channel_id=1, replica_groups=mesh['light'=8,'screen'=16] {'light'}, dimensions={0} | all-to-all | bytes 4194304 | tf_op jit(solution)/shard_map/all_to_all | solution.py:63
  255.0 4.3 %all-to-all-start.5 = ((f32[8,16,32,128]{3,2,1,0:T(8,128)}), f32[8,16,32,128]{3,2,1,0:T(8,128)}, u32[]{:S(2)}, u32[]{:S(2)}) async-start(f32[8,16,32,128]{3,2,1,0:T(8,128)} %get-tuple-element.8), calls=%async_computation.5 | async-start | bytes 4194304 | tf_op jit(solution)/shard_map/all_to_all | solution.py:63
  260.7 29.4 %all-to-all-done.5 = f32[8,16,32,128]{3,2,1,0:T(8,128)} async-done(((f32[8,16,32,128]{3,2,1,0:T(8,128)}), f32[8,16,32,128]{3,2,1,0:T(8,128)}, u32[]{:S(2)}, u32[]{:S(2)}) %all-to-all-start.5) | async-done | bytes 2097184 | tf_op jit(solution)/shard_map/all_to_all | solution.py:63
  290.1 4.8 %copy_bitcast_fusion = f32[32,32,1024]{2,1,0:T(8,128)} fusion(f32[8,16,32,128]{3,2,1,0:T(8,128)} %all-to-all-done.5, f32[8,16,32,128]{3,2,1,0:T(8,128)} %all_to_all.54), kind=kLoop, calls=%fused_computation.33 | loop fusion | flops 1048576 | bytes 8388608 | tf_op jit(solution)/shard_map/reshape | solution.py:54
  (35 shorter events, 4.3 us)
Async XLA Ops:
  0.6 49.4 %copy-start = (s32[512,1024]{1,0:T(8,128)S(1)}, s32[512,1024]{1,0:T(8,128)}, u32[]{:S(2)}) copy-start(s32[512,1024]{1,0:T(8,128)} %param.10) | copy-start | bytes 6291460
  11.2 40.6 %all-to-all-start.1 = ((f32[8,16,512]{2,1,0:T(8,128)}), f32[8,16,512]{2,1,0:T(8,128)S(1)}, u32[]{:S(2)}, u32[]{:S(2)}) async-start(f32[8,16,512]{2,1,0:T(8,128)} %broadcast_in_dim.29), calls=%async_computation.1 | async-start | bytes 524288 | tf_op jit(solution)/shard_map/all_to_all | solution.py:17
  43.3 6.8 %copy-start.6 = (f32[3,16]{1,0:T(4,128)S(1)}, f32[3,16]{1,0:T(4,128)}, u32[]{:S(2)}) copy-start(f32[3,16]{1,0:T(4,128)} %param.11) | copy-start | bytes 580
  47.2 23.9 %collective-permute-start = (f32[2,512,128]{2,1,0:T(8,128)}, f32[2,512,128]{2,1,0:T(8,128)S(1)}, u32[]{:S(2)}, u32[]{:S(2)}) collective-permute-start(f32[2,512,128]{2,1,0:T(8,128)} %slice.94), channel_id=1, source_target_pairs={{1,0},{2,1},{3,2},{4,3},{5,4},{6,5},{7,6},{8,7},{9,8},{10,9},{11,1... | collective-permute-start | bytes 1572872 | tf_op jit(solution)/shard_map/ppermute | solution.py:12
  58.3 4.5 %copy-start.4 = (f32[16,512,128]{2,1,0:T(8,128)}, f32[16,512,128]{2,1,0:T(8,128)S(1)}, u32[]{:S(2)}) copy-start(f32[16,512,128]{2,1,0:T(8,128)S(1)} %exponential_multiply_fusion) | copy-start | bytes 12582916
  62.7 50.7 %collective-permute-start.2 = (f32[2,512,128]{2,1,0:T(8,128)S(1)}, f32[2,512,128]{2,1,0:T(8,128)S(1)}, u32[]{:S(2)}, u32[]{:S(2)}) collective-permute-start(f32[2,512,128]{2,1,0:T(8,128)S(1)} %slice.133), channel_id=1, source_target_pairs={{1,0},{2,1},{3,2},{4,3},{5,4},{6,5},{7,6},{8,7},{9,8},{10,9},{11,1... | collective-permute-start | bytes 1572872 | tf_op jit(solution)/shard_map/ppermute | solution.py:12
  65.6 108.9 %all-to-all-start.3 = ((f32[16,512,128]{2,0,1:T(8,128)}), f32[16,512,128]{2,0,1:T(8,128)}, u32[]{:S(2)}, u32[]{:S(2)}) async-start(f32[16,512,128]{2,0,1:T(8,128)} %copy.36), calls=%async_computation.3 | async-start | bytes 8388608 | tf_op jit(solution)/shard_map/all_to_all | solution.py:162
  73.6 3.6 %copy-start.2 = (f32[18,512,128]{2,1,0:T(8,128)}, f32[18,512,128]{2,1,0:T(8,128)S(1)}, u32[]{:S(2)}) copy-start(f32[18,512,128]{2,1,0:T(8,128)S(1)} %pad_maximum_fusion) | copy-start | bytes 14155780
  84.2 23.4 %collective-permute-start.1 = (f32[18,514,1]{1,2,0:T(1,128)S(1)}, f32[18,514,1]{1,2,0:T(1,128)S(1)}, u32[]{:S(2)}, u32[]{:S(2)}) collective-permute-start(f32[18,514,1]{1,2,0:T(1,128)S(1)} %copy.30), channel_id=1, source_target_pairs={{16,0},{32,16},{48,32},{64,48},{80,64},{96,80},{112,96},{17,1},{33... | collective-permute-start | bytes 111032 | tf_op jit(solution)/shard_map/ppermute | solution.py:12
  116.0 3.5 %copy-start.3 = (f32[18,512,128]{2,1,0:T(8,128)}, f32[18,512,128]{2,1,0:T(8,128)S(1)}, u32[]{:S(2)}) copy-start(f32[18,512,128]{2,1,0:T(8,128)S(1)} %pad_maximum_fusion.1) | copy-start | bytes 14155780
  125.4 7.5 %collective-permute-start.3 = (f32[18,514,1]{1,2,0:T(1,128)S(1)}, f32[18,514,1]{1,2,0:T(1,128)S(1)}, u32[]{:S(2)}, u32[]{:S(2)}) collective-permute-start(f32[18,514,1]{1,2,0:T(1,128)S(1)} %copy.33), channel_id=1, source_target_pairs={{16,0},{32,16},{48,32},{64,48},{80,64},{96,80},{112,96},{17,1},{33... | collective-permute-start | bytes 111032 | tf_op jit(solution)/shard_map/ppermute | solution.py:12
  164.8 2.0 copy-start.5
  174.5 32.5 %all-to-all-start = ((f32[1,512,128]{2,0,1:T(1,128)}), f32[1,512,128]{2,0,1:T(1,128)S(1)}, u32[]{:S(2)}, u32[]{:S(2)}) async-start(f32[1,512,128]{2,0,1:T(1,128)} %bitcast.6), calls=%async_computation | async-start | bytes 524288 | tf_op jit(solution)/shard_map/all_to_all | solution.py:144
  206.9 11.2 %all-to-all-start.2 = ((f32[1,512,128]{2,0,1:T(1,128)}), f32[1,512,128]{2,0,1:T(1,128)S(1)}, u32[]{:S(2)}, u32[]{:S(2)}) async-start(f32[1,512,128]{2,0,1:T(1,128)} %bitcast.13), calls=%async_computation.2 | async-start | bytes 524288 | tf_op jit(solution)/shard_map/all_to_all | solution.py:143
  255.0 35.1 %all-to-all-start.5 = ((f32[8,16,32,128]{3,2,1,0:T(8,128)}), f32[8,16,32,128]{3,2,1,0:T(8,128)}, u32[]{:S(2)}, u32[]{:S(2)}) async-start(f32[8,16,32,128]{3,2,1,0:T(8,128)} %get-tuple-element.8), calls=%async_computation.5 | async-start | bytes 4194304 | tf_op jit(solution)/shard_map/all_to_all | solution.py:63
  259.3 35.6 %copy-start.1 = (s32[512,1024]{1,0:T(8,128)S(1)}, s32[512,1024]{1,0:T(8,128)}, u32[]{:S(2)}) copy-start(s32[512,1024]{1,0:T(8,128)} %param.10) | copy-start | bytes 6291460
where the time goes:
time: 296 us; the launch traced here: 295 us
  local copies, waits for them, and re-layouts  79.1 us (27%)
  other arithmetic  68 us (23%)
  starting transfers between devices  50.4 us (17%)
  waiting for transfers between devices  47.4 us (16%)
  blocking collectives  36.9 us (12%)
  matrix products  12.3 us (4%)
    all_to_all x1, blocking collectives, several_exchanges(): lax.all_to_all(piece, axis, split_axis=0, concat_axis=0, tiled=True)  36.9 us
    all_to_all x1, waiting for transfers between devices, several_exchanges(): lax.all_to_all(piece, axis, split_axis=0, concat_axis=0, tiled=True)  29.4 us
    add x1, other arithmetic, resample(): mixed = near + light_w * (further - near)  24.6 us
    reshape x1, local copies, waits for them, and re-layouts, local(): density.reshape(bricks_b, BRICK, bricks_a, BRICK, bricks_l, BRICK)  19.6 us
    all_to_all x1, starting transfers between devices, march_slabs(): lax.all_to_all(total[None], 'screen', split_axis=1, concat_axis=0, tiled=...  19.5 us
    ppermute x4, waiting for transfers between devices, passed_along(): return lax.ppermute(value, axis, pairs)  16.7 us
    slice x4, local copies, waits for them, and re-layouts, march_slabs(): tails = passed_along((dens_ext[:, :, :1], lit_ext[:, :, :1]), 'light', -1)  12 us
    concatenate x2, other arithmetic, march_slabs(): jnp.concatenate([masked, rims[0]], axis=0)  8.18 us
  transfers between devices with their start and end apart: 9, of which 4 were waited for; matrix products, arithmetic and copies ran while one was open for 48% of the time, Pallas kernels for 0%

commit v1 on v0

v1 whole, which is shorter than its diff:
```python
import jax
import jax.numpy as jnp
from jax import lax
from jax.experimental import pallas as pl
from jax.experimental.pallas import tpu as pltpu
from jax.sharding import PartitionSpec as P

MESH = pl.DeviceIdType.MESH
F32 = jnp.float32
BRICK = 16
SB = 16
NA = 512
LW = 128
PAD = 520
DS = (1, 3, 2)


def device(x, y, z, c):
    return (x * 2 + z // 2, y * 4 + (z % 2) * 2 + c)


def bcast(column, rows):
    return jnp.broadcast_to(column, (rows, LW))


def kernel(
    density, albedo, light_in, occ, phase, fractions,
    image_out, passing_out, bricks_out,
    fm, fl, gm, gl, big, w, mask, cform, tform, xbuf, tg, lin, ph, colsend, colrecv,
    img, imgr, img2, img2r, img3, img3r,
    din, ain, small, hs, hr, ts, tr, cs, cr, ys, yr, zs, zr, xs, xr, loc, i1s, i1r, i2s, i2r, i3s, i3r,
):
    li = lax.axis_index("light")
    sj = lax.axis_index("screen")
    x = li // 2
    zh = li % 2
    y = sj // 4
    zl = (sj // 2) % 2
    c = sj % 2
    z = zh * 2 + zl

    def remote(src, dst, ssem, rsem, dev):
        return pltpu.make_async_remote_copy(
            src_ref=src, dst_ref=dst, send_sem=ssem, recv_sem=rsem,
            device_id=dev, device_id_type=MESH,
        )

    def dload(b):
        return pltpu.make_async_copy(density.at[b], fm.at[b, pl.ds(0, NA)], din.at[b])

    def aload(b):
        return pltpu.make_async_copy(albedo.at[b], fl.at[b, pl.ds(0, NA)], ain.at[b])

    lcopy = pltpu.make_async_copy(light_in.at[pl.ds(sj * SB, SB)], lin, small.at[0])
    pcopy = pltpu.make_async_copy(phase.at[:, pl.ds(li * LW, LW)], ph, small.at[1])
    for b in range(SB):
        dload(b).start()
        aload(b).start()
    lcopy.start()
    pcopy.start()

    barrier = pltpu.get_barrier_semaphore()
    near = [(lax.rem(li + i, 8), sj) for i in range(1, 8)]
    near += [device(x, lax.rem(y + d, 4), z, c) for d in (1, 2, 3)]
    near += [device(lax.rem(x + d, 4), y, z, 1 - c) for d in range(4)]
    near += [device(x, y, lax.rem(z + d, 4), c) for d in (1, 2, 3)]
    near += [(li, lax.rem(sj + 1, 16)), (li, lax.rem(sj + 15, 16))]
    for dev in near:
        pl.semaphore_signal(barrier, inc=1, device_id=dev, device_id_type=MESH)

    lane = lax.broadcasted_iota(jnp.int32, (128, LW), 1)
    o = occ[0].astype(F32)
    spread = (
        lax.broadcasted_iota(jnp.int32, (8, LW), 1) // BRICK
        == lax.broadcasted_iota(jnp.int32, (8, LW), 0)
    ).astype(F32)
    wide = jnp.dot(o, spread, preferred_element_type=F32)
    tall = (
        lax.broadcasted_iota(jnp.int32, (NA, 32), 0) // BRICK
        == lax.broadcasted_iota(jnp.int32, (NA, 32), 1)
    ).astype(F32)
    mask[...] = jnp.dot(tall, wide, preferred_element_type=F32)
    r = lax.broadcasted_iota(jnp.int32, (256, 256), 0) % LW
    q = lax.broadcasted_iota(jnp.int32, (256, 256), 1)
    upper = jnp.logical_or(r < q, q >= LW).astype(jnp.bfloat16)

    zero8 = jnp.zeros((8, LW), F32)
    for b in range(SB + 1):
        for ref in (fm, fl, gm, gl):
            ref[b, NA:PAD, :] = zero8

    def first(b, _):
        dload(b).wait()
        aload(b).wait()
        for t in range(4):
            rows = pl.ds(t * 128, 128)
            m = fm[b, rows, :] * mask[rows, :]
            fm[b, rows, :] = m
            hi = m.astype(jnp.bfloat16)
            lo = (m - hi.astype(F32)).astype(jnp.bfloat16)
            both = jnp.dot(
                jnp.concatenate([hi, lo], axis=1), upper, preferred_element_type=F32
            )
            fl[b, rows, :] = fl[b, rows, :] * jnp.exp(-both[:, :LW])
            cform[0, rows, :] = jnp.where(lane == b, both[:, LW:], cform[0, rows, :])
        return 0

    lax.fori_loop(0, SB, first, 0)
    for t in range(4):
        cols = pl.ds(t * 128, 128)
        tg[li, :, cols] = cform[0, cols, :].T[:SB, :]

    pl.semaphore_wait(barrier, len(near))

    def tcopy(i):
        dev = (lax.rem(li + i, 8), sj)
        return remote(tg.at[li], tg.at[li], ts.at[i], tr.at[li], dev)

    for i in (4, 3, 5, 2, 6, 1, 7):
        tcopy(i).start()

    def halo(f, slot):
        return remote(
            f.at[0, pl.ds(0, NA)], f.at[SB, pl.ds(0, NA)], hs.at[slot], hr.at[slot],
            (li, lax.rem(sj + 15, 16)),
        )

    @pl.when(sj > 0)
    def _():
        halo(fm, 0).start()

    @pl.when(sj == 15)
    def _():
        for t in range(4):
            fm[SB, t * 128 : (t + 1) * 128, :] = jnp.zeros((128, LW), F32)
            fl[SB, t * 128 : (t + 1) * 128, :] = jnp.zeros((128, LW), F32)

    pcopy.wait()

    def weigh(t, _):
        rows = pl.ds(pl.multiple_of(t * 32, 32), 32)
        p = ph[rows, :]
        for k in range(3):
            v = jnp.full((32, LW), fractions[k, 0], F32)
            for level in range(1, 16):
                v = jnp.where(p == level, fractions[k, level], v)
            w[k, rows, :] = v
        return 0

    lax.fori_loop(0, 16, weigh, 0)
    xbuf[...] = jnp.zeros_like(xbuf)
    lcopy.wait()

    for i in range(1, 8):
        src = lax.rem(li + i, 8)
        remote(tg.at[src], tg.at[src], ts.at[i], tr.at[src], (src, sj)).wait_recv()
    before = jnp.zeros((SB, NA), F32)
    for i in range(8):
        before = before + jnp.where(i < li, tg[i], 0.0)
    xbuf[0:SB, :] = lin[...] * jnp.exp(-before)
    for t in range(4):
        cols = pl.ds(t * 128, 128)
        cform[0, cols, :] = xbuf[:, cols].T

    def unit(d, qq, kz):
        return (d * 4 + qq) * 2 + kz

    def held(d):
        return d if d == 0 else d + 3

    def ycopy(d, qq):
        return remote(
            big.at[pl.ds(unit(d, qq, 0), 2)], big.at[pl.ds(unit(d + 3, qq, 0), 2)],
            ys.at[d, qq], yr.at[d, qq], device(x, lax.rem(y + d, 4), z, c),
        )

    def zcopy(d, qq, kz):
        zz = 2 * zl + kz
        return zz, remote(
            big.at[unit(held(d), qq, kz)], big.at[56 + (zh * 4 + d) * 4 + qq],
            zs.at[d, qq, kz], zr.at[zh, d, qq], device(x, y, zz, c),
        )

    def zsend(d, qq):
        for kz in range(2):
            zz, cp = zcopy(d, qq, kz)

            @pl.when(zz != z)
            def _():
                cp.start()

    def mine(j):
        return (1 - (zl + zh) % 2) * (1 - (j + zh) % 2)

    def zwait(j, d, qq):
        @pl.when(mine(j) == 0)
        def _():
            place = big.at[56 + (j * 4 + d) * 4 + qq]
            remote(place, place, zs.at[d, qq, 0], zr.at[j, d, qq], device(x, y, z, 1 - c)).wait_recv()

    def xcopies(j, d, qq, kc):
        own = mine(j)
        at = own * unit(held(d), qq, zl) + (1 - own) * (56 + (j * 4 + d) * 4 + qq)
        src = big.at[at, pl.ds(kc * 128, 128)]
        slot = (x * 2 + j) * 2 + c
        xx = lax.rem(y + 4 - d, 4)
        here = jnp.logical_and(xx == x, c == kc)
        dst = bricks_out.at[slot, qq]
        far = remote(src, dst, xs.at[j, d, qq, kc], xr.at[slot, qq], device(xx, y, z, kc))
        near_ = pltpu.make_async_copy(src, dst, loc.at[j, qq])
        return here, near_, far

    def xsend(d, qq):
        for j in range(2):
            zwait(j, d, qq)
            for kc in range(2):
                here, near_, far = xcopies(j, d, qq, kc)

                @pl.when(here)
                def _():
                    near_.start()

                @pl.when(jnp.logical_not(here))
                def _():
                    far.start()

    for b in range(SB):
        qq, bb = b // 4, b % 4
        for d in range(4):
            yy = lax.rem(y + d, 4)
            rows = pl.ds(pl.multiple_of(yy * 128, 128), 128)
            v = fl[b, rows, :] * bcast(cform[0, rows, b : b + 1], 128)
            fl[b, rows, :] = v
            for k in range(4):
                big[unit(d, qq, k // 2), (k % 2) * 128 + bb * 32 : (k % 2) * 128 + bb * 32 + 32, :] = v[
                    k * 32 : k * 32 + 32, :
                ]
        if b == 0:
            @pl.when(sj > 0)
            def _():
                halo(fl, 1).start()
        if bb == 3:
            for d in DS:
                ycopy(d, qq).start()
            zsend(0, qq)

    def ystep(d, qq):
        place = big.at[pl.ds(unit(d + 3, qq, 0), 2)]
        remote(place, place, ys.at[d, qq], yr.at[d, qq], device(x, lax.rem(y + d, 4), z, c)).wait_recv()
        zsend(d, qq)

    def halo_wait():
        @pl.when(sj < 15)
        def _():
            for slot, f in enumerate((fm, fl)):
                place = f.at[SB, pl.ds(0, NA)]
                remote(place, place, hs.at[slot], hr.at[slot], (li, lax.rem(sj + 1, 16))).wait_recv()

    def ccopy():
        return remote(colsend, colrecv, cs, cr, (lax.rem(li + 7, 8), sj))

    def columns():
        for f, ref in enumerate((fm, fl)):
            def gather(t, _):
                rows = pl.ds(pl.multiple_of(t * 32, 32), 32)
                acc = jnp.zeros((32, LW), F32)
                for b in range(SB + 1):
                    acc = jnp.where(lane[:32] == b, bcast(ref[b, rows, 0:1], 32), acc)
                cform[f, rows, :] = acc
                return 0

            lax.fori_loop(0, 16, gather, 0)
            for t in range(4):
                cols = pl.ds(t * 128, 128)
                colsend[f, :, cols] = cform[f, cols, :].T[:24, :]

        @pl.when(li > 0)
        def _():
            ccopy().start()

        @pl.when(li == 7)
        def _():
            colrecv[...] = jnp.zeros_like(colrecv)

    def column_wait():
        @pl.when(li < 7)
        def _():
            remote(colrecv, colrecv, cs, cr, (lax.rem(li + 1, 8), sj)).wait_recv()
        for f in range(2):
            xbuf[0:24, :] = colrecv[f]
            for t in range(4):
                cols = pl.ds(t * 128, 128)
                cform[f, cols, :] = xbuf[:, cols].T

    def shifted(t, _):
        rows = pl.ds(pl.multiple_of(t * 32, 32), 32)
        for f, (src, dst) in enumerate(((fm, gm), (fl, gl))):
            edge = cform[f, rows, :]
            for b in range(SB + 1):
                rolled = pltpu.roll(src[b, rows, :], LW - 1, 1)
                dst[b, rows, :] = jnp.where(lane[:32] == LW - 1, bcast(edge[:, b : b + 1], 32), rolled)
        return 0

    def march(t, _):
        a0 = pl.multiple_of(t * 32, 32)
        rows = pl.ds(a0, 32)
        after = pl.ds(a0 + 1, 32)
        wb, wa, wl = w[0, rows, :], w[1, rows, :], w[2, rows, :]

        def mixed(f, g, b):
            f0 = f[b, rows, :]
            g0 = g[b, rows, :]
            near = f0 + wa * (f[b, after, :] - f0)
            further = g0 + wa * (g[b, after, :] - g0)
            return near + wl * (further - near)

        m0, s0 = mixed(fm, gm, 0), mixed(fl, gl, 0)
        passing = jnp.ones((32, LW), F32)
        part = jnp.zeros((32, LW), F32)
        for b in range(1, SB + 1):
            m1, s1 = mixed(fm, gm, b), mixed(fl, gl, b)
            extinct = m0 + wb * (m1 - m0)
            shaded = s0 + wb * (s1 - s0)
            left = passing * jnp.exp(-extinct)
            part = part + (passing - left) * shaded
            passing = left
            m0, s0 = m1, s1
        place = pl.ds(pl.multiple_of((t // 2) * 32, 32), 32)
        img[t % 2, 0, place, :] = part
        img[t % 2, 1, place, :] = passing
        return 0

    def joined(front, own, other):
        p0 = jnp.where(front, own[0], other[0])
        p1 = jnp.where(front, other[0], own[0])
        t0 = jnp.where(front, own[1], other[1])
        return p0 + t0 * p1, own[1] * other[1]

    def i1copy():
        return remote(img.at[1 - c], imgr, i1s, i1r, device(x, y, z, 1 - c))

    def i2copy():
        return remote(img2.at[1 - zl], img2r, i2s, i2r, device(x, y, zh * 2 + 1 - zl, c))

    def i3copy(d):
        yy = lax.rem(y + d, 4)
        return remote(img3.at[yy], img3r.at[y], i3s.at[d], i3r.at[y], device(x, yy, z, c))

    def image1():
        i1copy().wait_recv()
        for yy in range(4):
            for zz in range(2):
                rows = slice((yy * 2 + zz) * 32, (yy * 2 + zz) * 32 + 32)
                own = (img[c, 0, rows, :], img[c, 1, rows, :])
                a, t = joined(c == 0, own, (imgr[0, rows, :], imgr[1, rows, :]))
                img2[zz, 0, yy * 32 : yy * 32 + 32, :] = a
                img2[zz, 1, yy * 32 : yy * 32 + 32, :] = t
        i2copy().start()

    def image2():
        i2copy().wait_recv()
        for yy in range(4):
            rows = slice(yy * 32, yy * 32 + 32)
            own = (img2[zl, 0, rows, :], img2[zl, 1, rows, :])
            a, t = joined(zl == 0, own, (img2r[0, rows, :], img2r[1, rows, :]))
            img3[yy, 0, :, :] = a
            img3[yy, 1, :, :] = t
        for d in DS:
            i3copy(d).start()
        img3r[y] = img3[y]

    def image3():
        for d in DS:
            src = lax.rem(y + d, 4)
            remote(img3r.at[src], img3r.at[src], i3s.at[d], i3r.at[src], device(x, src, z, c)).wait_recv()
        a, t = img3r[0, 0], img3r[0, 1]
        for yy in range(1, 4):
            a = a + t * img3r[yy, 0]
            t = t * img3r[yy, 1]
        image_out[...] = a
        passing_out[...] = t

    def run(body, lo, hi):
        return lambda: lax.fori_loop(lo, hi, body, 0)

    work = {
        (0, 2): [halo_wait, columns],
        (1, 0): [column_wait, run(shifted, 0, 5)],
        (1, 1): [run(shifted, 5, 11)],
        (1, 2): [run(shifted, 11, 16)],
        (1, 3): [run(march, 0, 3)],
        (2, 0): [run(march, 3, 6)],
        (2, 1): [run(march, 6, 9)],
        (2, 2): [run(march, 9, 12)],
        (2, 3): [run(march, 12, 16), lambda: i1copy().start()],
        (3, 0): [image1],
        (3, 1): [image2],
        (3, 2): [image3],
    }
    order = [(qq, i) for qq in range(4) for i in range(4)]
    hops = (0,) + DS
    last = None
    for qq, i in order:
        if hops[i]:
            ystep(hops[i], qq)
        if last is not None:
            xsend(*last)
        last = (hops[i], qq)
        for task in work.get((qq, i), ()):
            task()
    xsend(*last)

    @pl.when(sj > 0)
    def _():
        halo(fm, 0).wait_send()
        halo(fl, 1).wait_send()

    for i in range(1, 8):
        tcopy(i).wait_send()

    @pl.when(li > 0)
    def _():
        ccopy().wait_send()

    i1copy().wait_send()
    i2copy().wait_send()
    for d in DS:
        i3copy(d).wait_send()
    for qq in range(4):
        for d in DS:
            ycopy(d, qq).wait_send()
        for d in range(4):
            for kz in range(2):
                zz, cp = zcopy(d, qq, kz)

                @pl.when(zz != z)
                def _():
                    cp.wait_send()

            for j in range(2):
                for kc in range(2):
                    here, near_, far = xcopies(j, d, qq, kc)

                    @pl.when(here)
                    def _():
                        near_.wait()

                    @pl.when(jnp.logical_not(here))
                    def _():
                        far.wait_send()

        for sx in range(4):
            for j in range(2):
                for sc in range(2):
                    slot = (sx * 2 + j) * 2 + sc
                    here = jnp.logical_and(sx == x, sc == c)

                    @pl.when(jnp.logical_not(here))
                    def _():
                        place = bricks_out.at[slot, qq]
                        remote(place, place, xs.at[0, 0, 0, 0], xr.at[slot, qq], device(x, y, z, 1 - c)).wait_recv()


def placed(src, out):
    out[...] = src[...].reshape(32, 32, LW)


def local(density, albedo, light_in, occupancy, phase, fractions):
    anywhere = pl.BlockSpec(memory_space=pl.ANY)
    vmem = pl.BlockSpec(memory_space=pltpu.VMEM)
    dma = pltpu.SemaphoreType.DMA
    image, passing, bricks = pl.pallas_call(
        kernel,
        out_shape=(
            jax.ShapeDtypeStruct((32, LW), F32),
            jax.ShapeDtypeStruct((32, LW), F32),
            jax.ShapeDtypeStruct((16, 4, 128, LW), F32),
        ),
        in_specs=[anywhere, anywhere, anywhere, vmem, anywhere, pl.BlockSpec(memory_space=pltpu.SMEM)],
        out_specs=(vmem, vmem, anywhere),
        scratch_shapes=[
            pltpu.VMEM((SB + 1, PAD, LW), F32),
            pltpu.VMEM((SB + 1, PAD, LW), F32),
            pltpu.VMEM((SB + 1, PAD, LW), F32),
            pltpu.VMEM((SB + 1, PAD, LW), F32),
            pltpu.VMEM((88, 256, LW), F32),
            pltpu.VMEM((3, NA, LW), F32),
            pltpu.VMEM((NA, LW), F32),
            pltpu.VMEM((2, NA, LW), F32),
            pltpu.VMEM((8, LW), F32),
            pltpu.VMEM((128, NA), F32),
            pltpu.VMEM((8, SB, NA), F32),
            pltpu.VMEM((SB, NA), F32),
            pltpu.VMEM((NA, LW), jnp.int32),
            pltpu.VMEM((2, 24, NA), F32),
            pltpu.VMEM((2, 24, NA), F32),
            pltpu.VMEM((2, 2, 256, LW), F32),
            pltpu.VMEM((2, 256, LW), F32),
            pltpu.VMEM((2, 2, 128, LW), F32),
            pltpu.VMEM((2, 128, LW), F32),
            pltpu.VMEM((4, 2, 32, LW), F32),
            pltpu.VMEM((4, 2, 32, LW), F32),
            dma((SB,)), dma((SB,)), dma((2,)),
            dma((2,)), dma((2,)), dma((8,)), dma((8,)), dma(()), dma(()),
            dma((4, 4)), dma((4, 4)), dma((4, 4, 2)), dma((2, 4, 4)),
            dma((2, 4, 4, 2)), dma((16, 4)), dma((2, 4)),
            dma(()), dma(()), dma(()), dma(()), dma((4,)), dma((4,)),
        ],
        compiler_params=pltpu.CompilerParams(
            collective_id=0, has_side_effects=True, vmem_limit_bytes=60 << 20
        ),
    )(density, albedo, light_in, occupancy, phase, fractions)
    bricks = bricks.reshape(16, 16, 32, LW)
    lit = pl.pallas_call(
        placed,
        grid=(8,),
        out_shape=jax.ShapeDtypeStruct((32, 32, 1024), F32),
        in_specs=[pl.BlockSpec((2, 16, 32, LW), lambda i: (i, 0, 0, 0))],
        out_specs=pl.BlockSpec((32, 32, LW), lambda i: (0, 0, i)),
    )(bricks)
    return image, passing, lit


def solution(mesh):
    return jax.shard_map(
        local,
        mesh=mesh,
        in_specs=(
            P("screen", None, "light"),
            P("screen", None, "light"),
            P(),
            P("screen", None, "light"),
            P(),
            P(),
        ),
        out_specs=(P("screen", "light"), P("screen", "light"), P("light", "screen", None)),
        check_vma=False,
    )
```

time: 296 us -> 112 us (0.38)
  the two profiles are of different devices: /device:TPU:8 before, /device:TPU:47 now
where the time goes in v1:
time: 112 us; the launch traced here: 111 us
  Pallas kernels  108 us (96%)
  local copies, waits for them, and re-layouts  2.59 us (2%)
    pallas_call x1, Pallas kernels, local(): pl.pallas_call(kernel, out_shape=(jax.ShapeDtypeStruct((32, LW), F32), ja...  101 us
    pallas_call x1, Pallas kernels, local(): pl.pallas_call(placed, grid=(8,), out_shape=jax.ShapeDtypeStruct((32, 32,...  6.59 us
    unnamed x7, local copies, waits for them, and re-layouts  2.59 us

profile of v1, /device:TPU:47, one launch (start us, length us, event | category | flops | bytes accessed | tf_op | source)
XLA Modules:
  0.0 111.3 jit_solution(13238271635706122074)
XLA Ops:
  0.6 1.4 %copy.9.occ = s32[1,32,8]{2,1,0:T(8,128)} copy(s32[1,32,8]{1,2,0:T(8,128)} %param.9) | data formatting | bytes 2048 | tf_op args[3]
  2.0 101.5 %shard_map.85 = (f32[32,128]{1,0:T(8,128)}, f32[32,128]{1,0:T(8,128)}, f32[16,4,128,128]{3,2,1,0:T(8,128)}) custom-call(f32[16,512,128]{2,1,0:T(8,128)} %density.1, f32[16,512,128]{2,1,0:T(8,128)} %albedo.1, f32[256,512]{1,0:T(8,128)} %light_in.1, s32[1,32,8]{2,1,0:T(8,128)} %copy.9.occ, s32[512,1024]{1,0:T(8,128)} %phase.1, f32[3,16]{1,0:T(4,128)} %fractions.1), custom_call_target="tpu_custom_call" | custom-call | tf_op jit(solution)/shard_map/pallas_call | solution.py:472
  103.5 0.0 copy-start.1
  103.5 0.0 copy-start
  103.5 6.6 %shard_map.86 = f32[32,32,1024]{2,1,0:T(8,128)} custom-call(f32[16,16,32,128]{3,2,1,0:T(8,128)} %bitcast.1), custom_call_target="tpu_custom_call" | custom-call | tf_op jit(solution)/shard_map/pallas_call | solution.py:514
  110.1 0.0 copy-done.1
  110.1 0.6 copy.12
  110.7 0.0 copy-done
  110.7 0.6 copy.13
Async XLA Ops:
  103.5 6.6 %copy-start.1 = (f32[32,128]{1,0:T(8,128)S(1)}, f32[32,128]{1,0:T(8,128)}, u32[]{:S(2)}) copy-start(f32[32,128]{1,0:T(8,128)} %get-tuple-element.12) | copy-start | bytes 49156
  103.5 7.2 %copy-start = (f32[32,128]{1,0:T(8,128)S(1)}, f32[32,128]{1,0:T(8,128)}, u32[]{:S(2)}) copy-start(f32[32,128]{1,0:T(8,128)} %get-tuple-element.13) | copy-start | bytes 49156

commit v2 on v1

v2 whole, which is shorter than its diff:
```python
import jax
import jax.numpy as jnp
from jax import lax
from jax.experimental import pallas as pl
from jax.experimental.pallas import tpu as pltpu
from jax.sharding import PartitionSpec as P

MESH = pl.DeviceIdType.MESH
F32 = jnp.float32
BRICK = 16
SB = 16
NA = 512
LW = 128
PAD = 520
DS = (1, 3, 2)
Q = 8
LAG = 5


def device(x, y, z, c):
    return (x * 2 + z // 2, y * 4 + (z % 2) * 2 + c)


def bcast(column, rows):
    return jnp.broadcast_to(column, (rows, LW))


def kernel(
    density, albedo, light_in, occ, phase, fractions,
    image_out, passing_out, factor_out, bricks_out,
    fm, fl, gm, gl, big, w, mask, cform, xbuf, cbuf, tg, lin, lin2, ph, colsend, colrecv,
    tb, tin, ftmp, img, imgr, img2, img2r, img3, img3r,
    din, ain, small, hs, hr, ts, tr, es, er, cs, cr, ys, yr, zs, zr, xs, xr, loc,
    tys, tyr, tzs, tzr, txs, txr, i1s, i1r, i2s, i2r, i3s, i3r,
):
    li = lax.axis_index("light")
    sj = lax.axis_index("screen")
    x = li // 2
    zh = li % 2
    y = sj // 4
    zl = (sj // 2) % 2
    c = sj % 2
    z = zh * 2 + zl

    def remote(src, dst, ssem, rsem, dev):
        return pltpu.make_async_remote_copy(
            src_ref=src, dst_ref=dst, send_sem=ssem, recv_sem=rsem,
            device_id=dev, device_id_type=MESH,
        )

    def dload(b):
        return pltpu.make_async_copy(density.at[b], fm.at[b, pl.ds(0, NA)], din.at[b])

    def aload(b):
        return pltpu.make_async_copy(albedo.at[b], fl.at[b, pl.ds(0, NA)], ain.at[b])

    lcopy = pltpu.make_async_copy(light_in.at[pl.ds(sj * SB, SB)], lin, small.at[0])
    pcopy = pltpu.make_async_copy(phase.at[:, pl.ds(li * LW, LW)], ph, small.at[1])
    l2copy = pltpu.make_async_copy(
        light_in.at[pl.ds(li * 32, 32), pl.ds(y * LW, LW)], lin2, small.at[2]
    )
    for b in range(SB):
        dload(b).start()
        aload(b).start()
    lcopy.start()
    l2copy.start()
    pcopy.start()

    barrier = pltpu.get_barrier_semaphore()
    near = [(lax.rem(li + i, 8), sj) for i in range(1, 8)]
    near += [device(x, lax.rem(y + d, 4), z, c) for d in (1, 2, 3)]
    near += [device(lax.rem(x + d, 4), y, z, 1 - c) for d in range(4)]
    near += [device(x, y, lax.rem(z + d, 4), c) for d in (1, 2, 3)]
    near += [(li, lax.rem(sj + 1, 16)), (li, lax.rem(sj + 15, 16))]
    for dev in near:
        pl.semaphore_signal(barrier, inc=1, device_id=dev, device_id_type=MESH)

    lane = lax.broadcasted_iota(jnp.int32, (128, LW), 1)
    o = occ[0].astype(F32)
    tall = (
        lax.broadcasted_iota(jnp.int32, (NA, 32), 0) // BRICK
        == lax.broadcasted_iota(jnp.int32, (NA, 32), 1)
    ).astype(F32)
    tall = lax.dot_general(tall, o, (((1,), (1,)), ((), ())), preferred_element_type=F32)
    spread = (
        lax.broadcasted_iota(jnp.int32, (8, LW), 1) // BRICK
        == lax.broadcasted_iota(jnp.int32, (8, LW), 0)
    ).astype(F32)
    mask[...] = jnp.dot(tall, spread, preferred_element_type=F32)
    r = lax.broadcasted_iota(jnp.int32, (256, 256), 0) % LW
    q = lax.broadcasted_iota(jnp.int32, (256, 256), 1)
    upper = jnp.logical_or(r < q, q >= LW).astype(jnp.bfloat16)

    def unit(d, qq, kz):
        return (d * Q + qq) * 2 + kz

    def held(d):
        return d if d == 0 else d + 3

    def middle(j, d, qq):
        return 14 * Q + (j * 4 + d) * Q + qq

    def ydev(d):
        return device(x, lax.rem(y + d, 4), z, c)

    def ycopy(d, qq):
        return remote(
            big.at[pl.ds(unit(d, qq, 0), 2)], big.at[pl.ds(unit(d + 3, qq, 0), 2)],
            ys.at[d, qq], yr.at[d, qq], ydev(d),
        )

    def ysend(qq):
        for d in DS:
            ycopy(d, qq).start()

    def halo(f, slot):
        return remote(
            f.at[0, pl.ds(0, NA)], f.at[SB, pl.ds(0, NA)], hs.at[slot], hr.at[slot],
            (li, lax.rem(sj + 15, 16)),
        )

    def first(qq):
        for bb in range(2):
            b = qq * 2 + bb
            dload(b).wait()
            aload(b).wait()
            for d in range(4):
                yy = lax.rem(y + d, 4)
                rows = pl.ds(pl.multiple_of(yy * 128, 128), 128)
                m = fm[b, rows, :] * mask[rows, :]
                fm[b, rows, :] = m
                hi = m.astype(jnp.bfloat16)
                lo = (m - hi.astype(F32)).astype(jnp.bfloat16)
                both = jnp.dot(
                    jnp.concatenate([hi, lo], axis=1), upper, preferred_element_type=F32
                )
                v = fl[b, rows, :] * jnp.exp(-both[:, :LW])
                fl[b, rows, :] = v
                for k in range(4):
                    to = (k % 2) * 64 + bb * 32
                    big[unit(d, qq, k // 2), to : to + 32, :] = v[k * 32 : k * 32 + 32, :]
                cform[0, rows, :] = jnp.where(lane == b, both[:, LW:], cform[0, rows, :])

    def weigh(t, _):
        rows = pl.ds(pl.multiple_of(t * 32, 32), 32)
        p = ph[rows, :]
        for k in range(3):
            v = jnp.full((32, LW), fractions[k, 0], F32)
            for level in range(1, 16):
                v = jnp.where(p == level, fractions[k, level], v)
            w[k, rows, :] = v
        return 0

    first(0)
    pcopy.wait()
    lax.fori_loop(0, 16, weigh, 0)
    pl.semaphore_wait(barrier, len(near))
    @pl.when(sj > 0)
    def _():
        halo(fm, 0).start()
        halo(fl, 1).start()

    ysend(0)
    first(1)
    ysend(1)

    @pl.when(sj == 15)
    def _():
        for t in range(4):
            fm[SB, t * 128 : (t + 1) * 128, :] = jnp.zeros((128, LW), F32)
            fl[SB, t * 128 : (t + 1) * 128, :] = jnp.zeros((128, LW), F32)
        xbuf[SB:24, :] = jnp.zeros((8, NA), F32)

    first(2)

    def rest(qq, _):
        first(qq)
        return 0

    lax.fori_loop(3, Q, rest, 0)
    for t in range(4):
        cols = pl.ds(t * 128, 128)
        totals = cform[0, cols, :].T[:SB, :]
        tg[li, :, cols] = totals
        tb[lax.rem(t + 4 - y, 4)] = totals

    def tcopy(i):
        dev = (lax.rem(li + i, 8), sj)
        return remote(tg.at[li], tg.at[li], ts.at[i], tr.at[li], dev)

    def tycopy(d):
        return remote(tb.at[d], tb.at[d + 3], tys.at[d], tyr.at[d], ydev(d))

    for i in (4, 3, 5, 2, 6, 1, 7):
        tcopy(i).start()
    for d in DS:
        tycopy(d).start()

    zero8 = jnp.zeros((8, LW), F32)
    for b in range(SB + 1):
        for ref in (fm, fl, gm, gl):
            ref[b, NA:PAD, :] = zero8

    def zcopy(d, qq, kz):
        zz = 2 * zl + kz
        return zz, remote(
            big.at[unit(held(d), qq, kz)], big.at[middle(zh, d, qq)],
            zs.at[d, qq, kz], zr.at[zh, d, qq], device(x, y, zz, c),
        )

    def tzcopy(d, kz):
        zz = 2 * zl + kz
        return zz, remote(
            tb.at[held(d)], tb.at[7 + zh * 4 + d], tzs.at[d, kz], tzr.at[zh, d],
            device(x, y, zz, c),
        )

    def zsend(d, qq):
        for kz in range(2):
            zz, cp = zcopy(d, qq, kz)

            @pl.when(zz != z)
            def _():
                cp.start()

    def mine(j):
        return (1 - (zl + zh) % 2) * (1 - (j + zh) % 2)

    def zwait(j, d, qq):
        @pl.when(mine(j) == 0)
        def _():
            place = big.at[middle(j, d, qq)]
            remote(place, place, zs.at[d, qq, 0], zr.at[j, d, qq], device(x, y, z, 1 - c)).wait_recv()

    def xto(j, d, kc):
        xx = lax.rem(y + 4 - d, 4)
        here = jnp.logical_and(xx == x, c == kc)
        return (x * 2 + j) * 2 + c, here, device(xx, y, z, kc)

    def xcopies(j, d, qq, kc):
        own = mine(j)
        at = own * unit(held(d), qq, zl) + (1 - own) * middle(j, d, qq)
        src = big.at[at, pl.ds(kc * 64, 64)]
        slot, here, dev = xto(j, d, kc)
        dst = bricks_out.at[slot, qq]
        far = remote(src, dst, xs.at[j, d, qq, kc], xr.at[slot, qq], dev)
        near_ = pltpu.make_async_copy(src, dst, loc.at[j, qq])
        return here, near_, far

    def xsend(d, qq):
        for j in range(2):
            zwait(j, d, qq)
            for kc in range(2):
                here, near_, far = xcopies(j, d, qq, kc)

                @pl.when(here)
                def _():
                    near_.start()

                @pl.when(jnp.logical_not(here))
                def _():
                    far.start()

    def ystep(d, qq):
        if d:
            place = big.at[pl.ds(unit(d + 3, qq, 0), 2)]
            remote(place, place, ys.at[d, qq], yr.at[d, qq], ydev(d)).wait_recv()
        zsend(d, qq)

    def totals_z():
        for d in DS:
            remote(tb.at[d + 3], tb.at[d + 3], tys.at[d], tyr.at[d], ydev(d)).wait_recv()
        for d in range(4):
            for kz in range(2):
                zz, cp = tzcopy(d, kz)

                @pl.when(zz != z)
                def _():
                    cp.start()

    def txcopy(j, d, kc):
        own = mine(j)
        at = own * held(d) + (1 - own) * (7 + j * 4 + d)
        slot, here, dev = xto(j, d, kc)
        return at, slot, here, remote(tb.at[at], tin.at[slot], txs.at[j, d, kc], txr.at[slot], dev)

    def totals_x():
        for j in range(2):
            for d in range(4):
                @pl.when(mine(j) == 0)
                def _():
                    place = tb.at[7 + j * 4 + d]
                    remote(place, place, tzs.at[d, 0], tzr.at[j, d], device(x, y, z, 1 - c)).wait_recv()

                for kc in range(2):
                    at, slot, here, far = txcopy(j, d, kc)

                    @pl.when(here)
                    def _():
                        tin[slot] = tb[at]

                    @pl.when(jnp.logical_not(here))
                    def _():
                        far.start()

    def arrivals(wait):
        for sx in range(4):
            for j in range(2):
                for sc in range(2):
                    slot = (sx * 2 + j) * 2 + sc
                    here = jnp.logical_and(sx == x, sc == c)

                    @pl.when(jnp.logical_not(here))
                    def _():
                        wait(slot)

    def factors():
        def wait(slot):
            remote(tin.at[slot], tin.at[slot], txs.at[0, 0, 0], txr.at[slot], device(x, y, z, 1 - c)).wait_recv()

        arrivals(wait)
        l2copy.wait()
        for cc in range(2):
            above = jnp.zeros((SB, LW), F32)
            for i in range(8):
                ftmp[i * SB : i * SB + SB, :] = lin2[cc * SB : cc * SB + SB, :] * jnp.exp(-above)
                above = above + tin[i * 2 + cc]
            cform[0, 0:128, :] = ftmp[...].T
            factor_out[cc] = cform[0, pl.ds(pl.multiple_of((zl * 2 + c) * 32, 32), 32), :]

    def ecopy():
        return remote(
            xbuf.at[pl.ds(0, 8)], xbuf.at[pl.ds(SB, 8)], es, er, (li, lax.rem(sj + 15, 16))
        )

    def reach():
        lcopy.wait()
        for i in range(1, 8):
            src = lax.rem(li + i, 8)
            remote(tg.at[src], tg.at[src], ts.at[i], tr.at[src], (src, sj)).wait_recv()
        before = jnp.zeros((SB, NA), F32)
        for i in range(8):
            before = before + jnp.where(i < li, tg[i], 0.0)
        xbuf[0:SB, :] = lin[...] * jnp.exp(-before)

        @pl.when(sj > 0)
        def _():
            ecopy().start()

    def halo_wait():
        @pl.when(sj > 0)
        def _():
            halo(fm, 0).wait_send()
            halo(fl, 1).wait_send()

        @pl.when(sj < 15)
        def _():
            for slot, f in enumerate((fm, fl)):
                place = f.at[SB, pl.ds(0, NA)]
                remote(place, place, hs.at[slot], hr.at[slot], (li, lax.rem(sj + 1, 16))).wait_recv()
            place = xbuf.at[pl.ds(SB, 8)]
            remote(place, place, es, er, (li, lax.rem(sj + 1, 16))).wait_recv()

        for t in range(4):
            cols = pl.ds(t * 128, 128)
            cform[0, cols, :] = xbuf[:, cols].T

    def scale(t, _):
        rows = pl.ds(pl.multiple_of(t * 32, 32), 32)
        e = cform[0, rows, :]
        am = jnp.zeros((32, LW), F32)
        al = jnp.zeros((32, LW), F32)
        for b in range(SB + 1):
            v = fl[b, rows, :] * bcast(e[:, b : b + 1], 32)
            fl[b, rows, :] = v
            al = jnp.where(lane[:32] == b, bcast(v[:, 0:1], 32), al)
            am = jnp.where(lane[:32] == b, bcast(fm[b, rows, 0:1], 32), am)
        cform[1, rows, :] = am
        cform[2, rows, :] = al
        return 0

    def ccopy():
        return remote(colsend, colrecv, cs, cr, (lax.rem(li + 7, 8), sj))

    def columns():
        for f in range(2):
            for t in range(4):
                cols = pl.ds(t * 128, 128)
                colsend[f, :, cols] = cform[f + 1, cols, :].T[:24, :]

        @pl.when(li > 0)
        def _():
            ccopy().start()

        @pl.when(li == 7)
        def _():
            colrecv[...] = jnp.zeros_like(colrecv)

    def column_wait():
        @pl.when(li < 7)
        def _():
            remote(colrecv, colrecv, cs, cr, (lax.rem(li + 1, 8), sj)).wait_recv()
        for f in range(2):
            cbuf[0:24, :] = colrecv[f]
            for t in range(4):
                cols = pl.ds(t * 128, 128)
                cform[f + 1, cols, :] = cbuf[:, cols].T

    def shifted(t, _):
        rows = pl.ds(pl.multiple_of(t * 32, 32), 32)
        for f, (src, dst) in enumerate(((fm, gm), (fl, gl))):
            edge = cform[f + 1, rows, :]
            for b in range(SB + 1):
                rolled = pltpu.roll(src[b, rows, :], LW - 1, 1)
                dst[b, rows, :] = jnp.where(lane[:32] == LW - 1, bcast(edge[:, b : b + 1], 32), rolled)
        return 0

    def march(t, _):
        a0 = pl.multiple_of(t * 32, 32)
        rows = pl.ds(a0, 32)
        after = pl.ds(a0 + 1, 32)
        wb, wa, wl = w[0, rows, :], w[1, rows, :], w[2, rows, :]

        def mixed(f, g, b):
            f0 = f[b, rows, :]
            g0 = g[b, rows, :]
            near_ = f0 + wa * (f[b, after, :] - f0)
            further = g0 + wa * (g[b, after, :] - g0)
            return near_ + wl * (further - near_)

        m0, s0 = mixed(fm, gm, 0), mixed(fl, gl, 0)
        passing = jnp.ones((32, LW), F32)
        part = jnp.zeros((32, LW), F32)
        for b in range(1, SB + 1):
            m1, s1 = mixed(fm, gm, b), mixed(fl, gl, b)
            extinct = m0 + wb * (m1 - m0)
            shaded = s0 + wb * (s1 - s0)
            left = passing * jnp.exp(-extinct)
            part = part + (passing - left) * shaded
            passing = left
            m0, s0 = m1, s1
        place = pl.ds(pl.multiple_of((t // 2) * 32, 32), 32)
        img[t % 2, 0, place, :] = part
        img[t % 2, 1, place, :] = passing
        return 0

    def joined(front, own, other):
        p0 = jnp.where(front, own[0], other[0])
        p1 = jnp.where(front, other[0], own[0])
        t0 = jnp.where(front, own[1], other[1])
        return p0 + t0 * p1, own[1] * other[1]

    def i1copy():
        return remote(img.at[1 - c], imgr, i1s, i1r, device(x, y, z, 1 - c))

    def i2copy():
        return remote(img2.at[1 - zl], img2r, i2s, i2r, device(x, y, zh * 2 + 1 - zl, c))

    def i3copy(d):
        yy = lax.rem(y + d, 4)
        return remote(img3.at[yy], img3r.at[y], i3s.at[d], i3r.at[y], device(x, yy, z, c))

    def image1():
        i1copy().wait_recv()
        for yy in range(4):
            for zz in range(2):
                rows = slice((yy * 2 + zz) * 32, (yy * 2 + zz) * 32 + 32)
                own = (img[c, 0, rows, :], img[c, 1, rows, :])
                a, t = joined(c == 0, own, (imgr[0, rows, :], imgr[1, rows, :]))
                img2[zz, 0, yy * 32 : yy * 32 + 32, :] = a
                img2[zz, 1, yy * 32 : yy * 32 + 32, :] = t
        i2copy().start()

    def image2():
        i2copy().wait_recv()
        for yy in range(4):
            rows = slice(yy * 32, yy * 32 + 32)
            own = (img2[zl, 0, rows, :], img2[zl, 1, rows, :])
            a, t = joined(zl == 0, own, (img2r[0, rows, :], img2r[1, rows, :]))
            img3[yy, 0, :, :] = a
            img3[yy, 1, :, :] = t
        for d in DS:
            i3copy(d).start()
        img3r[y] = img3[y]

    def image3():
        for d in DS:
            src = lax.rem(y + d, 4)
            remote(img3r.at[src], img3r.at[src], i3s.at[d], i3r.at[src], device(x, src, z, c)).wait_recv()
        a, t = img3r[0, 0], img3r[0, 1]
        for yy in range(1, 4):
            a = a + t * img3r[yy, 0]
            t = t * img3r[yy, 1]
        image_out[...] = a
        passing_out[...] = t

    def run(body, lo, hi):
        return lambda: lax.fori_loop(lo, hi, body, 0)

    work = {
        (2, 1): [reach],
        (3, 0): [totals_z],
        (3, 3): [halo_wait],
        (4, 0): [run(scale, 0, 4)],
        (4, 1): [run(scale, 4, 8)],
        (4, 2): [run(scale, 8, 12)],
        (4, 3): [run(scale, 12, 16), columns],
        (5, 0): [totals_x],
        (5, 2): [column_wait],
        (5, 3): [run(shifted, 0, 4)],
        (6, 0): [run(shifted, 4, 8)],
        (6, 1): [run(shifted, 8, 12)],
        (6, 2): [run(shifted, 12, 16)],
        (6, 3): [run(march, 0, 4)],
        (7, 0): [run(march, 4, 8)],
        (7, 1): [run(march, 8, 12)],
        (7, 2): [run(march, 12, 16), lambda: i1copy().start()],
    }
    late = []
    for qq in range(Q):
        for i, d in enumerate((0,) + DS):
            ystep(d, qq)
            late.append((d, qq))
            if len(late) > LAG:
                xsend(*late.pop(0))
            if i == 3 and qq + 2 < Q:
                ysend(qq + 2)
            for task in work.get((qq, i), ()):
                task()
    for item in late:
        xsend(*item)
    image1()
    factors()
    image2()
    image3()

    for i in range(1, 8):
        tcopy(i).wait_send()

    @pl.when(sj > 0)
    def _():
        ecopy().wait_send()

    @pl.when(li > 0)
    def _():
        ccopy().wait_send()

    i1copy().wait_send()
    i2copy().wait_send()
    for d in DS:
        i3copy(d).wait_send()
        tycopy(d).wait_send()
    for d in range(4):
        for kz in range(2):
            zz, cp = tzcopy(d, kz)

            @pl.when(zz != z)
            def _():
                cp.wait_send()

        for j in range(2):
            for kc in range(2):
                at, slot, here, far = txcopy(j, d, kc)

                @pl.when(jnp.logical_not(here))
                def _():
                    far.wait_send()

    def ended(qq, _):
        for d in DS:
            ycopy(d, qq).wait_send()
        for d in range(4):
            for kz in range(2):
                zz, cp = zcopy(d, qq, kz)

                @pl.when(zz != z)
                def _():
                    cp.wait_send()

            for j in range(2):
                for kc in range(2):
                    here, near_, far = xcopies(j, d, qq, kc)

                    @pl.when(here)
                    def _():
                        near_.wait()

                    @pl.when(jnp.logical_not(here))
                    def _():
                        far.wait_send()

        def wait(slot):
            place = bricks_out.at[slot, qq]
            remote(place, place, xs.at[0, 0, 0, 0], xr.at[slot, qq], device(x, y, z, 1 - c)).wait_recv()

        arrivals(wait)
        return 0

    lax.fori_loop(0, Q, ended, 0)


def placed(src, factor, image, passing, out, image_out, passing_out, came, goes, rs, ws):
    def read(i):
        return pltpu.make_async_copy(src.at[:, i // 4, pl.ds((i % 4) * 4, 4)], came.at[i], rs.at[i])

    def write(i):
        return pltpu.make_async_copy(goes.at[i], out.at[pl.ds(i * 4, 4)], ws.at[i])

    for i in range(8):
        read(i).start()
    image_out[...] = image[...]
    passing_out[...] = passing[...]

    def step(i, _):
        read(i).wait()
        f = pltpu.roll(factor[i // 4], lax.rem(LW - (i % 4) * 4, LW), 1)
        for b in range(4):
            for s in range(8):
                at = s * SB + b
                goes[i, b, :, s * LW : (s + 1) * LW] = came[i, s, b] * bcast(f[:, at : at + 1], 32)
        write(i).start()
        return 0

    lax.fori_loop(0, 8, step, 0)
    for i in range(8):
        write(i).wait()


def local(density, albedo, light_in, occupancy, phase, fractions):
    anywhere = pl.BlockSpec(memory_space=pl.ANY)
    vmem = pl.BlockSpec(memory_space=pltpu.VMEM)
    dma = pltpu.SemaphoreType.DMA
    tile = jax.ShapeDtypeStruct((32, LW), F32)
    image, passing, factor, bricks = pl.pallas_call(
        kernel,
        out_shape=(
            tile,
            tile,
            jax.ShapeDtypeStruct((2, 32, LW), F32),
            jax.ShapeDtypeStruct((16, Q, 64, LW), F32),
        ),
        in_specs=[anywhere, anywhere, anywhere, vmem, anywhere, pl.BlockSpec(memory_space=pltpu.SMEM)],
        out_specs=(vmem, vmem, vmem, anywhere),
        scratch_shapes=[
            pltpu.VMEM((SB + 1, PAD, LW), F32),
            pltpu.VMEM((SB + 1, PAD, LW), F32),
            pltpu.VMEM((SB + 1, PAD, LW), F32),
            pltpu.VMEM((SB + 1, PAD, LW), F32),
            pltpu.VMEM((22 * Q, 128, LW), F32),
            pltpu.VMEM((3, NA, LW), F32),
            pltpu.VMEM((NA, LW), F32),
            pltpu.VMEM((3, NA, LW), F32),
            pltpu.VMEM((128, NA), F32),
            pltpu.VMEM((128, NA), F32),
            pltpu.VMEM((8, SB, NA), F32),
            pltpu.VMEM((SB, NA), F32),
            pltpu.VMEM((32, LW), F32),
            pltpu.VMEM((NA, LW), jnp.int32),
            pltpu.VMEM((2, 24, NA), F32),
            pltpu.VMEM((2, 24, NA), F32),
            pltpu.VMEM((15, SB, LW), F32),
            pltpu.VMEM((16, SB, LW), F32),
            pltpu.VMEM((128, LW), F32),
            pltpu.VMEM((2, 2, 256, LW), F32),
            pltpu.VMEM((2, 256, LW), F32),
            pltpu.VMEM((2, 2, 128, LW), F32),
            pltpu.VMEM((2, 128, LW), F32),
            pltpu.VMEM((4, 2, 32, LW), F32),
            pltpu.VMEM((4, 2, 32, LW), F32),
            dma((SB,)), dma((SB,)), dma((3,)),
            dma((2,)), dma((2,)), dma((8,)), dma((8,)), dma(()), dma(()), dma(()), dma(()),
            dma((4, Q)), dma((4, Q)), dma((4, Q, 2)), dma((2, 4, Q)),
            dma((2, 4, Q, 2)), dma((16, Q)), dma((2, Q)),
            dma((4,)), dma((4,)), dma((4, 2)), dma((2, 4)), dma((2, 4, 2)), dma((16,)),
            dma(()), dma(()), dma(()), dma(()), dma((4,)), dma((4,)),
        ],
        compiler_params=pltpu.CompilerParams(
            collective_id=0, has_side_effects=True, vmem_limit_bytes=60 << 20
        ),
    )(density, albedo, light_in, jnp.swapaxes(occupancy, 1, 2), phase, fractions)
    bricks = bricks.reshape(8, 2, 16, 32, LW)
    lit, image, passing = pl.pallas_call(
        placed,
        out_shape=(jax.ShapeDtypeStruct((32, 32, 1024), F32), tile, tile),
        in_specs=[anywhere, vmem, vmem, vmem],
        out_specs=(anywhere, vmem, vmem),
        scratch_shapes=[
            pltpu.VMEM((8, 8, 4, 32, LW), F32),
            pltpu.VMEM((8, 4, 32, 1024), F32),
            dma((8,)),
            dma((8,)),
        ],
    )(bricks, factor, image, passing)
    return image, passing, lit


def solution(mesh):
    return jax.shard_map(
        local,
        mesh=mesh,
        in_specs=(
            P("screen", None, "light"),
            P("screen", None, "light"),
            P(),
            P("screen", None, "light"),
            P(),
            P(),
        ),
        out_specs=(P("screen", "light"), P("screen", "light"), P("light", "screen", None)),
        check_vma=False,
    )
```

time: 112 us -> 104 us (0.929)
  the two profiles are of different devices: /device:TPU:47 before, /device:TPU:8 now
where the time goes in v2:
time: 104 us; the launch traced here: 103 us
  Pallas kernels  103 us (99%)
    pallas_call x1, Pallas kernels, local(): pl.pallas_call(kernel, out_shape=(tile, tile, jax.ShapeDtypeStruct((2, 32...  96.7 us
    pallas_call x1, Pallas kernels, local(): pl.pallas_call(placed, out_shape=(jax.ShapeDtypeStruct((32, 32, 1024), F3...  5.97 us

profile of v2, /device:TPU:8, one launch (start us, length us, event | category | flops | bytes accessed | tf_op | source)
XLA Modules:
  0.0 103.3 jit_solution(14472882404384693251)
XLA Ops:
  0.6 96.7 %shard_map.85 = (f32[32,128]{1,0:T(8,128)}, f32[32,128]{1,0:T(8,128)}, f32[2,32,128]{2,1,0:T(8,128)}, f32[16,8,64,128]{3,2,1,0:T(8,128)}) custom-call(f32[16,512,128]{2,1,0:T(8,128)} %density.1, f32[16,512,128]{2,1,0:T(8,128)} %albedo.1, f32[256,512]{1,0:T(8,128)} %light_in.1, s32[1,8,32]{2,1,0:T(8,128)} %bitcast.3, s32[512,1024]{1,0:T(8,128)} %phase.1, ...), custom_call_target="tpu_custom_call" | custom-call | tf_op jit(solution)/shard_map/pallas_call | solution.py:634
  97.3 6.0 %shard_map.86 = (f32[32,32,1024]{2,1,0:T(8,128)}, f32[32,128]{1,0:T(8,128)}, f32[32,128]{1,0:T(8,128)}) custom-call(f32[8,2,16,32,128]{4,3,2,1,0:T(8,128)} %bitcast.2, f32[2,32,128]{2,1,0:T(8,128)} %get-tuple-element.11.factor, f32[32,128]{1,0:T(8,128)} %get-tuple-element.12.image, f32[32,128]{1,0:T(8,128)} %get-tuple-element.13.passing), custom_call_target="tpu_custom_call" | custom-call | tf_op jit(solution)/shard_map/pallas_call | solution.py:682

commit v3 on v2

--- a/solution.py
+++ b/solution.py
@@ -505,16 +505,16 @@
         (4, 1): [run(scale, 4, 8)],
         (4, 2): [run(scale, 8, 12)],
         (4, 3): [run(scale, 12, 16), columns],
-        (5, 0): [totals_x],
-        (5, 2): [column_wait],
-        (5, 3): [run(shifted, 0, 4)],
-        (6, 0): [run(shifted, 4, 8)],
-        (6, 1): [run(shifted, 8, 12)],
-        (6, 2): [run(shifted, 12, 16)],
-        (6, 3): [run(march, 0, 4)],
-        (7, 0): [run(march, 4, 8)],
-        (7, 1): [run(march, 8, 12)],
-        (7, 2): [run(march, 12, 16), lambda: i1copy().start()],
+        (5, 0): [totals_x, column_wait],
+        (5, 1): [run(shifted, 0, 4)],
+        (5, 2): [run(shifted, 4, 8)],
+        (5, 3): [run(shifted, 8, 12)],
+        (6, 0): [run(shifted, 12, 16)],
+        (6, 1): [run(march, 0, 4)],
+        (6, 2): [run(march, 4, 8)],
+        (6, 3): [run(march, 8, 12)],
+        (7, 0): [run(march, 12, 16), lambda: i1copy().start()],
+        (7, 2): [image1],
     }
     late = []
     for qq in range(Q):
@@ -529,9 +529,8 @@
                 task()
     for item in late:
         xsend(*item)
-    image1()
+    image2()
     factors()
-    image2()
     image3()
 
     for i in range(1, 8):

time: 104 us -> 106 us (1.019)
    pallas_call x1, Pallas kernels: 96.7 us -> 98.5 us  [local(): pl.pallas_call(kernel, out_shape=(tile, tile, jax.ShapeDtypeStruct((2, 32...]
where the time goes in v3:
time: 106 us; the launch traced here: 105 us
  Pallas kernels  104 us (98%)
    pallas_call x1, Pallas kernels, local(): pl.pallas_call(kernel, out_shape=(tile, tile, jax.ShapeDtypeStruct((2, 32...  98.5 us
    pallas_call x1, Pallas kernels, local(): pl.pallas_call(placed, out_shape=(jax.ShapeDtypeStruct((32, 32, 1024), F3...  5.97 us

profile of v3, /device:TPU:8, one launch (start us, length us, event | category | flops | bytes accessed | tf_op | source)
XLA Modules:
  0.0 105.1 jit_solution(13305933997686657858)
XLA Ops:
  0.6 98.5 %shard_map.85 = (f32[32,128]{1,0:T(8,128)}, f32[32,128]{1,0:T(8,128)}, f32[2,32,128]{2,1,0:T(8,128)}, f32[16,8,64,128]{3,2,1,0:T(8,128)}) custom-call(f32[16,512,128]{2,1,0:T(8,128)} %density.1, f32[16,512,128]{2,1,0:T(8,128)} %albedo.1, f32[256,512]{1,0:T(8,128)} %light_in.1, s32[1,8,32]{2,1,0:T(8,128)} %bitcast.3, s32[512,1024]{1,0:T(8,128)} %phase.1, ...), custom_call_target="tpu_custom_call" | custom-call | tf_op jit(solution)/shard_map/pallas_call | solution.py:633
  99.1 6.0 %shard_map.86 = (f32[32,32,1024]{2,1,0:T(8,128)}, f32[32,128]{1,0:T(8,128)}, f32[32,128]{1,0:T(8,128)}) custom-call(f32[8,2,16,32,128]{4,3,2,1,0:T(8,128)} %bitcast.2, f32[2,32,128]{2,1,0:T(8,128)} %get-tuple-element.11.factor, f32[32,128]{1,0:T(8,128)} %get-tuple-element.12.image, f32[32,128]{1,0:T(8,128)} %get-tuple-element.13.passing), custom_call_target="tpu_custom_call" | custom-call | tf_op jit(solution)/shard_map/pallas_call | solution.py:681
